TPU v7x, 32 devices: a whole 2x2x4 slice. The times are simulated.
32 devices in a mesh: group: 2 (over y), tm: 4 (over z), bl: 2 (over x), pol: 2 (over core).
Axes of the slice: x: 2, y: 2, z: 4, core: 2. Of those that a mesh axis runs over, the one named last changes fastest.
Arguments:
- visibilities: bfloat16 [1600, 256, 2, 384], P(('group', 'tm'), ('bl', 'pol')), parts along dimension 0, may hold values from -6 to 6
- flag_mask: int32 [1600], P(('group', 'tm')), parts along dimension 0, may hold values 0 or 1
- kernel_index: int32 [256], P(('bl', 'pol')), may hold values from 0 to 15
- filter_bank: float32 [2, 16, 257], replicated, may hold values from -0.875 to 0.875
Outputs:
- fringe_filtered: bfloat16 [160, 256, 2, 384], P('group', ('bl', 'pol', 'tm')), parts along dimension 0
There are 2 independent parts, one for each index of `group`. A program takes and returns all parts, laid end to end along the dimension named above; an argument that names none is the same for every part. Nothing has to cross between parts.
All inputs are finite; a program needn't handle non-finite values. No bound on the sum of `flag_mask` on one device may be relied on, other than what follows from the above.
Results may differ from a plain program's by a relative error of at most 0.001.
Values may be sent and summed in bfloat16 or wider, within the bound.
No kernel may reach another device: no remote copies, remote signals or barrier semaphores. Data moves between devices by JAX's collectives and lax.ppermute only.
A program may use at most 192 MiB of HBM per device.

v0:
```python
import jax
import jax.numpy as jnp
from jax import lax
from jax.sharding import PartitionSpec as P

TAPS = 257
AVG = 10


def padded(block, sides, width):
    for axis, dim in sides:
        count = lax.axis_size(axis)
        forward = [(i, i + 1) for i in range(count - 1)]
        backward = [(target, source) for source, target in forward]
        low = lax.ppermute(
            lax.slice_in_dim(block, block.shape[dim] - width, None, axis=dim), axis, forward
        )
        high = lax.ppermute(lax.slice_in_dim(block, 0, width, axis=dim), axis, backward)
        block = jnp.concatenate([low, block, high], axis=dim)
    return block


def select_taps(kernel_index, filter_bank):
    choices_count = filter_bank.shape[1]
    one_hot = (kernel_index[:, None] == jnp.arange(choices_count, dtype=jnp.int32)[None, :]).astype(
        jnp.float32
    )
    return jnp.einsum("bk,rkt->brt", one_hot, filter_bank, precision=lax.Precision.HIGHEST)


def make_band(kernel_taps, block_rows):
    tap_count = kernel_taps.shape[1]
    row_width = block_rows + tap_count - 1
    zero_tail = jnp.zeros((2, block_rows), jnp.float32)
    period_row = jnp.concatenate([kernel_taps, zero_tail], axis=1)
    tiled_rows = jnp.tile(period_row, (1, block_rows))[:, : block_rows * row_width]
    return tiled_rows.reshape(2, block_rows, row_width)


def filter_block(time_slab, kernel_taps, block_rows):
    band_rows = make_band(kernel_taps, block_rows)
    row_width = band_rows.shape[2]
    band_rows = band_rows.reshape(2, block_rows // AVG, AVG, row_width).sum(axis=2) * (1.0 / AVG)
    out_count = band_rows.shape[1]
    stacked = band_rows.reshape(2 * out_count, row_width)
    product = jnp.dot(
        stacked, time_slab, precision=lax.Precision.HIGHEST, preferred_element_type=jnp.float32
    )
    prod_real = product[:out_count]
    prod_imag = product[out_count:]
    channels = time_slab.shape[1] // 2
    out_real = prod_real[:, :channels] - prod_imag[:, channels:]
    out_imag = prod_real[:, channels:] + prod_imag[:, :channels]
    result = jnp.stack([out_real, out_imag], axis=1)
    return result


def per_device(visibilities, flag_mask, kernel_index, filter_bank):
    half_taps = TAPS // 2
    block_rows = visibilities.shape[0]
    masked = visibilities * flag_mask.astype(jnp.bfloat16)[:, None, None, None]
    extended = padded(masked, (("tm", 0),), half_taps)
    taps_all = select_taps(kernel_index, filter_bank)

    def per_base(base_index):
        time_slab = lax.dynamic_index_in_dim(extended, base_index, 1, False).astype(jnp.float32)
        time_slab = time_slab.reshape(extended.shape[0], -1)
        kernel_taps = lax.dynamic_index_in_dim(taps_all, base_index, 0, False)
        return filter_block(time_slab, kernel_taps, block_rows)

    filtered = lax.map(per_base, jnp.arange(visibilities.shape[1], dtype=jnp.int32))
    averaged = jnp.moveaxis(filtered, 0, 1).astype(jnp.bfloat16)
    return lax.all_to_all(averaged, "tm", split_axis=1, concat_axis=0, tiled=True)


def solution(mesh):
    placed = (
        P(("group", "tm"), ("bl", "pol"), None, None),
        P(("group", "tm")),
        P(("bl", "pol")),
        P(),
    )
    return jax.shard_map(
        per_device,
        mesh=mesh,
        in_specs=placed,
        out_specs=P("group", ("bl", "pol", "tm"), None, None),
        check_vma=False,
    )
```

profile of v0, /device:TPU:0, one launch (start us, length us, event | category | flops | bytes accessed | tf_op | source)
XLA Modules:
  0.0 985.1 jit_solution(15027337351065907888)
XLA Ops:
  0.7 25.5 %broadcast_multiply_fusion.1 = bf16[200,64,2,384]{3,2,1,0:T(2,128)(2,1)S(1)} fusion(bf16[200,64,2,384]{3,2,1,0:T(2,128)(2,1)} %param.6, bf16[200]{0:T(256)(128)(2,1)S(1)} %convert_element_type.11), kind=kLoop, calls=%fused_computation.11 | loop fusion | flops 9830400 | bytes 39322000 | tf_op jit(solution)/shard_map/mul | solution.py:61
  26.2 23.1 %fusion.6 = (bf16[128,64,2,384]{3,2,1,0:T(2,128)(2,1)}, bf16[128,64,2,384]{3,2,1,0:T(2,128)(2,1)}) fusion(bf16[200,64,2,384]{3,2,1,0:T(2,128)(2,1)S(1)} %broadcast_multiply_fusion.1), kind=kLoop, calls=%fused_computation.17 | loop fusion | bytes 50331648 | tf_op jit(solution)/shard_map/slice | solution.py:16
  49.3 9.5 collective-permute-start
  60.4 263.7 %collective-permute-done = bf16[128,64,2,384]{3,2,1,0:T(2,128)(2,1)} collective-permute-done((bf16[128,64,2,384]{3,2,1,0:T(2,128)(2,1)}, bf16[128,64,2,384]{3,2,1,0:T(2,128)(2,1)}, u32[]{:S(2)}, u32[]{:S(2)}) %collective-permute-start) | collective-permute-done | bytes 12582944 | tf_op jit(solution)/shard_map/ppermute | solution.py:15
  324.2 8.7 collective-permute-done.1
  332.8 69.3 %pad_maximum_fusion = bf16[456,64,2,384]{3,2,1,0:T(2,128)(2,1)} fusion(bf16[128,64,2,384]{3,2,1,0:T(2,128)(2,1)} %collective-permute-done.1, bf16[200,64,2,384]{3,2,1,0:T(2,128)(2,1)} %copy-done.2, bf16[128,64,2,384]{3,2,1,0:T(2,128)(2,1)} %collective-permute-done), kind=kLoop, calls=%fused_computation.10 | loop fusion | flops 44826624 | bytes 89653248 | tf_op jit(solution)/shard_map/concatenate | solution.py:19
  402.2 532.0 %while.10 = (s32[]{:T(128)}, bf16[64,20,2,384]{3,2,1,0:T(2,128)(2,1)}, s32[64]{0:T(128)S(1)}, f32[64,2,257]{2,0,1:T(8,128)S(1)}, bf16[456,64,2,384]{3,2,1,0:T(2,...) while((s32[]{:T(128)}, bf16[64,20,2,384]{3,2,1,0:T(2,128)(2,1)}, s32[64]{0:T(128)S(1)}, ...), condition=%wide.region_2.3_spmd, body=%wide.region_0.2_spmd.sunk | while | flops 168328320 | bytes 10199059 | solution.py:71
  407.7 1.6 constant_dynamic-slice_fusion.5
  416.0 1.6 constant_dynamic-slice_fusion.5
  424.3 1.6 constant_dynamic-slice_fusion.5
  432.6 1.6 constant_dynamic-slice_fusion.5
  440.9 1.6 constant_dynamic-slice_fusion.5
  449.2 1.6 constant_dynamic-slice_fusion.5
  457.5 1.6 constant_dynamic-slice_fusion.5
  465.8 1.6 constant_dynamic-slice_fusion.5
  474.1 1.6 constant_dynamic-slice_fusion.5
  482.5 1.6 constant_dynamic-slice_fusion.5
  490.8 1.6 constant_dynamic-slice_fusion.5
  499.1 1.6 constant_dynamic-slice_fusion.5
  507.4 1.6 constant_dynamic-slice_fusion.5
  515.7 1.6 constant_dynamic-slice_fusion.5
  524.0 1.6 constant_dynamic-slice_fusion.5
  532.3 1.6 constant_dynamic-slice_fusion.5
  540.6 1.6 constant_dynamic-slice_fusion.5
  549.0 1.6 constant_dynamic-slice_fusion.5
  557.3 1.6 constant_dynamic-slice_fusion.5
  565.6 1.6 constant_dynamic-slice_fusion.5
  573.9 1.6 constant_dynamic-slice_fusion.5
  582.2 1.6 constant_dynamic-slice_fusion.5
  590.5 1.6 constant_dynamic-slice_fusion.5
  598.8 1.6 constant_dynamic-slice_fusion.5
  607.1 1.6 constant_dynamic-slice_fusion.5
  615.4 1.6 constant_dynamic-slice_fusion.5
  623.8 1.6 constant_dynamic-slice_fusion.5
  632.1 1.6 constant_dynamic-slice_fusion.5
  640.4 1.6 constant_dynamic-slice_fusion.5
  690.3 1.6 constant_dynamic-slice_fusion.5
  698.6 1.6 constant_dynamic-slice_fusion.5
  706.9 1.6 constant_dynamic-slice_fusion.5
  715.2 1.6 constant_dynamic-slice_fusion.5
  723.5 1.6 constant_dynamic-slice_fusion.5
  848.2 1.6 constant_dynamic-slice_fusion.5
  856.5 1.6 constant_dynamic-slice_fusion.5
  864.8 1.6 constant_dynamic-slice_fusion.5
  873.1 1.6 constant_dynamic-slice_fusion.5
  881.4 1.6 constant_dynamic-slice_fusion.5
  934.1 48.2 %all_to_all.18 = bf16[20,64,2,384]{3,2,0,1:T(2,128)(2,1)S(1)} all-to-all(bf16[20,64,2,384]{3,2,0,1:T(2,128)(2,1)} %bitcast.45), channel_id=1, replica_groups=mesh['group'=2,'tm'=4,'bl'=2,'pol'=2] {'tm'}, dimensions={1} | all-to-all | bytes 3932160 | tf_op jit(solution)/shard_map/all_to_all | solution.py:73
  982.4 2.8 copy.11
  (1062 shorter events, 336.0 us)
Async XLA Ops:
  0.0 60.1 %copy-start = (f32[2,16,257]{2,1,0:T(8,128)S(1)}, f32[2,16,257]{2,1,0:T(8,128)}, u32[]{:S(2)}) copy-start(f32[2,16,257]{2,1,0:T(8,128)} %param.9) | copy-start | bytes 98692
  26.2 23.1 %copy-start.2 = (bf16[200,64,2,384]{3,2,1,0:T(2,128)(2,1)}, bf16[200,64,2,384]{3,2,1,0:T(2,128)(2,1)S(1)}, u32[]{:S(2)}) copy-start(bf16[200,64,2,384]{3,2,1,0:T(2,128)(2,1)S(1)} %broadcast_multiply_fusion.1) | copy-start | bytes 58982404
  26.2 33.9 %copy-start.3 = (s32[64]{0:T(128)S(1)}, s32[64]{0:T(128)}, u32[]{:S(2)}) copy-start(s32[64]{0:T(128)} %param.8) | copy-start | bytes 772
  49.3 274.9 %collective-permute-start = (bf16[128,64,2,384]{3,2,1,0:T(2,128)(2,1)}, bf16[128,64,2,384]{3,2,1,0:T(2,128)(2,1)}, u32[]{:S(2)}, u32[]{:S(2)}) collective-permute-start(bf16[128,64,2,384]{3,2,1,0:T(2,128)(2,1)} %get-tuple-element.60), channel_id=1, source_target_pairs={{0,4},{4,8},{8,12},{1,5},{5,9},{9,13},{2,6},{6,10},{10,14},{3,7},{... | collective-permute-start | bytes 37748744 | tf_op jit(solution)/shard_map/ppermute | solution.py:15
  58.8 274.0 %collective-permute-start.1 = (bf16[128,64,2,384]{3,2,1,0:T(2,128)(2,1)}, bf16[128,64,2,384]{3,2,1,0:T(2,128)(2,1)}, u32[]{:S(2)}, u32[]{:S(2)}) collective-permute-start(bf16[128,64,2,384]{3,2,1,0:T(2,128)(2,1)} %get-tuple-element.61), channel_id=1, source_target_pairs={{4,0},{8,4},{12,8},{5,1},{9,5},{13,9},{6,2},{10,6},{14,10},{7,3},{... | collective-permute-start | bytes 37748744 | tf_op jit(solution)/shard_map/ppermute | solution.py:18
  934.1 51.0 %copy-start.1 = (f32[2,16,257]{2,1,0:T(8,128)S(1)}, f32[2,16,257]{2,1,0:T(8,128)}, u32[]{:S(2)}) copy-start(f32[2,16,257]{2,1,0:T(8,128)} %param.9) | copy-start | bytes 98692
where the time goes:
time: 990 us; the launch traced here: 985 us
  local copies, waits for them, and re-layouts  373 us (38%)
  waiting for transfers between devices  272 us (27%)
  loops' own time  136 us (14%)
  other arithmetic  115 us (12%)
  blocking collectives  48.2 us (5%)
  matrix products  29 us (3%)
  starting transfers between devices  10.8 us (1%)
    ppermute x1, waiting for transfers between devices, padded(): lax.ppermute(lax.slice_in_dim(block, block.shape[dim] - width, None, axis...  264 us
    another operation x1, loops' own time, per_device(): lax.map(per_base, jnp.arange(visibilities.shape[1], dtype=jnp.int32))  136 us
    dynamic_slice x64, local copies, waits for them, and re-layouts, per_base(): lax.dynamic_index_in_dim(extended, base_index, 1, False).astype(jnp.float32)  102 us
    another operation x128, local copies, waits for them, and re-layouts, make_band(): jnp.tile(period_row, (1, block_rows))[:, :block_rows * row_width]  78.5 us
    reshape x64, local copies, waits for them, and re-layouts, filter_block(): band_rows.reshape(2, block_rows // AVG, AVG, row_width).sum(axis=2)  73.2 us
    concatenate x1, other arithmetic, padded(): block = jnp.concatenate([low, block, high], axis=dim)  69.3 us
    all_to_all x1, blocking collectives, per_device(): lax.all_to_all(averaged, 'tm', split_axis=1, concat_axis=0, tiled=True)  48.2 us
    dynamic_slice x64, local copies, waits for them, and re-layouts, per_device(): lax.map(per_base, jnp.arange(visibilities.shape[1], dtype=jnp.int32))  41.2 us
  transfers between devices with their start and end apart: 2, of which 2 were waited for; matrix products, arithmetic and copies ran while one was open for 0% of the time, Pallas kernels for 0%

commit v1 on v0

v1 whole, which is shorter than its diff:
```python
import functools

import jax
import jax.numpy as jnp
from jax import lax
from jax.experimental import pallas as pl
from jax.experimental.pallas import tpu as pltpu
from jax.sharding import PartitionSpec as P

TAPS = 257
AVG = 10
HALF = TAPS // 2
HALO = -(-HALF // AVG)


def round_up(value, step):
    return -(-value // step) * step


def line_pair(filter_bank, rows, lines):
    summed = sum(
        jnp.pad(filter_bank, ((0, 0), (0, 0), (j, AVG - 1 - j))) for j in range(AVG)
    ) * (1.0 / AVG)
    real, imag = summed[0], summed[1]
    pair = jnp.stack(
        [jnp.stack([real, -imag], axis=-1), jnp.stack([imag, real], axis=-1)], axis=1
    )
    pair = pair.reshape(real.shape[0], 2, 2 * real.shape[1])
    period = round_up(2 * rows + 2 * AVG * lines, 128)
    split = 2 * (AVG * HALO + HALF)
    gap = jnp.zeros(pair.shape[:2] + (period - pair.shape[2],), jnp.float32)
    return jnp.concatenate([pair[:, :, split:], gap, pair[:, :, :split]], axis=2)


def bank_body(lines_ref, flags_ref, bank_ref, *, lines, width):
    for part in range(2):
        row = lines_ref[0, part : part + 1, :]
        spread = jnp.broadcast_to(row, (8, row.shape[1]))
        tiles = []
        for tile in range(lines // 8):
            shifted = pltpu.roll(spread, 2 * AVG * 8 * tile, 1)
            shifted = pltpu.roll(shifted, 0, 1, stride=AVG, stride_axis=0)
            tiles.append(pltpu.roll(shifted, 0, 1, stride=AVG, stride_axis=0)[:, :width])
        band = jnp.concatenate(tiles, axis=0)
        band = band * flags_ref[...]
        high = band.astype(jnp.bfloat16)
        low = (band - high.astype(jnp.float32)).astype(jnp.bfloat16)
        bank_ref[0, part * lines : (part + 1) * lines, :] = high
        bank_ref[0, (2 + part) * lines : (3 + part) * lines, :] = low


def main_body(index_ref, vis_ref, bank_ref, out_ref, *, group, half):
    step = pl.program_id(0)
    rows, _, _, chans = vis_ref.shape
    for i in range(group):
        band = bank_ref[index_ref[step * group + i]]
        slab = vis_ref[:, i, :, :].reshape(2 * rows, chans)
        prod = jnp.dot(band, slab, preferred_element_type=jnp.float32)
        out_ref[i] = prod[:half] + prod[half:]


def partial_rows(visibilities, flag_mask, kernel_index, filter_bank):
    rows, bases, _, chans = visibilities.shape
    kernels = filter_bank.shape[1]
    lines = round_up(rows // AVG + 2 * HALO, 8)
    width = 2 * rows
    pairs = line_pair(filter_bank, rows, lines)
    flags = jnp.repeat(flag_mask.astype(jnp.float32), 2)[None, :]
    bank = pl.pallas_call(
        functools.partial(bank_body, lines=lines, width=width),
        grid=(kernels,),
        in_specs=[
            pl.BlockSpec((1, 2, pairs.shape[2]), lambda k: (k, 0, 0)),
            pl.BlockSpec((1, width), lambda k: (0, 0)),
        ],
        out_specs=pl.BlockSpec((1, 4 * lines, width), lambda k: (k, 0, 0)),
        out_shape=jax.ShapeDtypeStruct((kernels, 4 * lines, width), jnp.bfloat16),
        name="bank",
    )(pairs, flags)
    group = 8 if bases % 8 == 0 else 1
    return pl.pallas_call(
        functools.partial(main_body, group=group, half=2 * lines),
        grid_spec=pltpu.PrefetchScalarGridSpec(
            num_scalar_prefetch=1,
            grid=(bases // group,),
            in_specs=[
                pl.BlockSpec((rows, group, 2, chans), lambda g, _: (0, g, 0, 0)),
                pl.BlockSpec(bank.shape, lambda g, _: (0, 0, 0)),
            ],
            out_specs=pl.BlockSpec((group, 2 * lines, chans), lambda g, _: (g, 0, 0)),
        ),
        out_shape=jax.ShapeDtypeStruct((bases, 2 * lines, chans), jnp.float32),
        compiler_params=pltpu.CompilerParams(vmem_limit_bytes=50 * 1024 * 1024),
        name="partials",
    )(kernel_index, visibilities, bank)


def per_device(visibilities, flag_mask, kernel_index, filter_bank):
    rows, bases, _, chans = visibilities.shape
    own = rows // AVG
    prod = partial_rows(visibilities, flag_mask, kernel_index, filter_bank)
    prod = prod.reshape(bases, 2, prod.shape[1] // 2, chans)
    prod = jnp.transpose(prod, (2, 0, 1, 3))
    count = lax.axis_size("tm")
    up = [(i, i + 1) for i in range(count - 1)]
    down = [(i + 1, i) for i in range(count - 1)]
    from_low = lax.ppermute(prod[own + HALO : own + 2 * HALO], "tm", up)
    from_high = lax.ppermute(prod[:HALO], "tm", down)
    total = prod[HALO : HALO + own]
    total = total + jnp.pad(from_low, ((0, own - HALO), (0, 0), (0, 0), (0, 0)))
    total = total + jnp.pad(from_high, ((own - HALO, 0), (0, 0), (0, 0), (0, 0)))
    averaged = total.astype(jnp.bfloat16)
    return lax.all_to_all(averaged, "tm", split_axis=1, concat_axis=0, tiled=True)


def solution(mesh):
    placed = (
        P(("group", "tm"), ("bl", "pol"), None, None),
        P(("group", "tm")),
        P(("bl", "pol")),
        P(),
    )
    return jax.shard_map(
        per_device,
        mesh=mesh,
        in_specs=placed,
        out_specs=P("group", ("bl", "pol", "tm"), None, None),
        check_vma=False,
    )
```

time: 990 us -> 161 us (0.16)
  local copies, waits for them, and re-layouts: 373 us -> 19.1 us
  waiting for transfers between devices: 272 us -> 57.3 us
  loops' own time: 136 us -> 0 us
  other arithmetic: 115 us -> 2.76 us
  matrix products: 29 us -> 0 us
  Pallas kernels: 0 us -> 26.5 us
    ppermute x2, waiting for transfers between devices: 272 us -> 57.3 us  [the longest x1 53.1 us: per_device(): from_low = lax.ppermute(prod[own + HALO:own + 2 * HALO], 'tm', up)]
    dynamic_slice x256 -> x0, local copies, waits for them, and re-layouts: 144 us -> none  [the longest x64 102 us: per_base(): lax.dynamic_index_in_dim(extended, base_index, 1, False).astype(jnp.float32)]
    another operation x1 -> x0, loops' own time: 136 us -> none  [per_device(): lax.map(per_base, jnp.arange(visibilities.shape[1], dtype=jnp.int32))]
    another operation x128 -> x7, local copies, waits for them, and re-layouts: 78.5 us -> 1.72 us  [the longest x1 0.69 us: partial_rows(): flags = jnp.repeat(flag_mask.astype(jnp.float32), 2)[None, :]]
    concatenate x1 -> x0, other arithmetic: 69.3 us -> none  [padded(): block = jnp.concatenate([low, block, high], axis=dim)]
    reshape x64 -> x1, local copies, waits for them, and re-layouts: 73.2 us -> 9.14 us  [per_device(): prod = prod.reshape(bases, 2, prod.shape[1] // 2, chans)]
    dynamic_update_slice x64 -> x0, local copies, waits for them, and re-layouts: 41 us -> none  [per_device(): lax.map(per_base, jnp.arange(visibilities.shape[1], dtype=jnp.int32))]
    dot_general x65 -> x0, matrix products: 29 us -> none  [the longest x64 28.7 us: filter_block(): jnp.dot(stacked, time_slab, precision=lax.Precision.HIGHEST, preferred_el...]
where the time goes in v1:
time: 161 us; the launch traced here: 160 us
  waiting for transfers between devices  57.3 us (36%)
  blocking collectives  47.8 us (30%)
  Pallas kernels  26.5 us (16%)
  local copies, waits for them, and re-layouts  19.1 us (12%)
  starting transfers between devices  6.59 us (4%)
  other arithmetic  2.76 us (2%)
    ppermute x1, waiting for transfers between devices, per_device(): from_low = lax.ppermute(prod[own + HALO:own + 2 * HALO], 'tm', up)  53.1 us
    all_to_all x1, blocking collectives, per_device(): lax.all_to_all(averaged, 'tm', split_axis=1, concat_axis=0, tiled=True)  47.8 us
    pallas_call x1, Pallas kernels, partial_rows(): pl.pallas_call(functools.partial(main_body, group=group, half=2 * lines),...  16 us
    pallas_call x1, Pallas kernels, partial_rows(): pl.pallas_call(functools.partial(bank_body, lines=lines, width=width), gr...  10.5 us
    reshape x1, local copies, waits for them, and re-layouts, per_device(): prod = prod.reshape(bases, 2, prod.shape[1] // 2, chans)  9.14 us
    ppermute x1, starting transfers between devices, per_device(): from_low = lax.ppermute(prod[own + HALO:own + 2 * HALO], 'tm', up)  5.12 us
    ppermute x1, waiting for transfers between devices, per_device(): from_high = lax.ppermute(prod[:HALO], 'tm', down)  4.28 us
  transfers between devices with their start and end apart: 2, of which 2 were waited for; matrix products, arithmetic and copies ran while one was open for 0% of the time, Pallas kernels for 0%

profile of v1, /device:TPU:0, one launch (start us, length us, event | category | flops | bytes accessed | tf_op | source)
XLA Modules:
  0.0 160.2 jit_solution(17636874027039236561)
XLA Ops:
  0.0 0.0 copy-start.2
  0.0 1.6 add_multiply_fusion
  1.6 0.2 copy.13
  1.8 0.2 stack.17
  2.0 0.1 copy.15
  2.1 0.2 copy.14
  2.3 0.0 copy-start.1
  2.4 0.2 stack.19
  2.6 0.1 copy.16
  2.7 0.1 pad_maximum_fusion.3
  2.8 0.1 pad_maximum_fusion
  2.9 0.0 copy-done.2
  2.9 0.1 broadcast_in_dim.7
  3.0 0.7 broadcast_in_dim_reshape.3.flags_ref
  3.7 1.1 concatenate.4.lines_ref
  4.8 10.5 %bank.1.bank_ref = bf16[16,192,400]{2,1,0:T(8,128)(2,1)} custom-call(f32[16,2,1408]{2,1,0:T(2,128)} %concatenate.4.lines_ref, f32[1,400]{1,0:T(1,128)} %broadcast_in_dim_reshape.3.flags_ref), custom_call_target="tpu_custom_call" | custom-call | tf_op jit(solution)/shard_map/bank/pallas_call | solution.py:69
  15.3 0.0 copy-done.1
  15.3 0.0 copy-start
  15.3 1.9 %copy-done = bf16[16,192,400]{2,1,0:T(8,128)(2,1)S(1)} copy-done((bf16[16,192,400]{2,1,0:T(8,128)(2,1)S(1)}, bf16[16,192,400]{2,1,0:T(8,128)(2,1)}, u32[]{:S(2)}) %copy-start) | copy-done | bytes 2457624
  17.2 16.0 %partials.1 = f32[64,96,384]{2,1,0:T(8,128)} custom-call(s32[64]{0:T(128)S(1)} %copy-done.1, bf16[200,64,2,384]{3,2,1,0:T(2,128)(2,1)} %vis_ref.1, bf16[16,192,400]{2,1,0:T(8,128)(2,1)S(1)} %copy-done), custom_call_target="tpu_custom_call" | custom-call | tf_op jit(solution)/shard_map/partials/pallas_call | solution.py:81
  33.2 9.1 %copy.21 = f32[64,2,48,384]{3,0,1,2:T(8,128)S(1)} copy(f32[64,2,48,384]{3,2,1,0:T(8,128)} %bitcast.18) | data formatting | bytes 18874368 | tf_op jit(solution)/shard_map/reshape | solution.py:102
  42.4 0.3 fusion.3
  42.7 5.1 %collective-permute-start = (f32[13,64,2,384]{3,1,2,0:T(8,128)S(1)}, f32[13,64,2,384]{3,1,2,0:T(8,128)S(1)}, u32[]{:S(2)}, u32[]{:S(2)}) collective-permute-start(f32[13,64,2,384]{3,1,2,0:T(8,128)S(1)} %get-tuple-element.5), channel_id=1, source_target_pairs={{0,4},{4,8},{8,12},{1,5},{5,9},{9,13},{2,6},{6,10},{10,14},{3,7},{... | collective-permute-start | bytes 7667720 | tf_op jit(solution)/shard_map/ppermute | solution.py:107
  47.9 1.5 collective-permute-start.1
  49.3 53.1 %collective-permute-done = f32[13,64,2,384]{3,1,2,0:T(8,128)S(1)} collective-permute-done((f32[13,64,2,384]{3,1,2,0:T(8,128)S(1)}, f32[13,64,2,384]{3,1,2,0:T(8,128)S(1)}, u32[]{:S(2)}, u32[]{:S(2)}) %collective-permute-start) | collective-permute-done | bytes 2555936 | tf_op jit(solution)/shard_map/ppermute | solution.py:107
  102.4 4.3 %collective-permute-done.1 = f32[13,64,2,384]{3,1,2,0:T(8,128)S(1)} collective-permute-done((f32[13,64,2,384]{3,1,2,0:T(8,128)S(1)}, f32[13,64,2,384]{3,1,2,0:T(8,128)S(1)}, u32[]{:S(2)}, u32[]{:S(2)}) %collective-permute-start.1) | collective-permute-done | bytes 2555936 | tf_op jit(solution)/shard_map/ppermute | solution.py:108
  106.7 1.0 fusion.1
  107.7 2.0 %copy.18 = bf16[20,64,2,384]{3,2,0,1:T(2,128)(2,1)S(1)} copy(bf16[20,64,2,384]{3,1,2,0:T(8,128)(2,1)S(1)} %fusion.1) | data formatting | bytes 3932160 | tf_op jit(solution)/shard_map/convert_element_type | solution.py:112
  109.7 47.8 %all_to_all.18 = bf16[20,64,2,384]{3,2,0,1:T(2,128)(2,1)S(1)} all-to-all(bf16[20,64,2,384]{3,2,0,1:T(2,128)(2,1)S(1)} %copy.18), channel_id=1, replica_groups=mesh['group'=2,'tm'=4,'bl'=2,'pol'=2] {'tm'}, dimensions={1} | all-to-all | bytes 3932160 | tf_op jit(solution)/shard_map/all_to_all | solution.py:113
  157.4 2.8 %copy.19 = bf16[4,20,16,2,384]{4,3,2,1,0:T(2,128)(2,1)} copy(bf16[4,20,16,2,384]{4,3,1,2,0:T(2,128)(2,1)S(1)} %bitcast.21) | data formatting | bytes 3932160 | tf_op jit(solution)/shard_map/all_to_all | solution.py:113
  (5 shorter events, 0.1 us)
Async XLA Ops:
  0.0 2.9 %copy-start.2 = (s32[200]{0:T(256)S(1)}, s32[200]{0:T(256)}, u32[]{:S(2)}) copy-start(s32[200]{0:T(256)} %param.5) | copy-start | bytes 2404
  2.3 13.0 %copy-start.1 = (s32[64]{0:T(128)S(1)}, s32[64]{0:T(128)}, u32[]{:S(2)}) copy-start(s32[64]{0:T(128)} %index_ref.1) | copy-start | bytes 772
  15.3 1.9 %copy-start = (bf16[16,192,400]{2,1,0:T(8,128)(2,1)S(1)}, bf16[16,192,400]{2,1,0:T(8,128)(2,1)}, u32[]{:S(2)}) copy-start(bf16[16,192,400]{2,1,0:T(8,128)(2,1)} %bank.1.bank_ref) | copy-start | bytes 7372804
  42.7 59.7 %collective-permute-start = (f32[13,64,2,384]{3,1,2,0:T(8,128)S(1)}, f32[13,64,2,384]{3,1,2,0:T(8,128)S(1)}, u32[]{:S(2)}, u32[]{:S(2)}) collective-permute-start(f32[13,64,2,384]{3,1,2,0:T(8,128)S(1)} %get-tuple-element.5), channel_id=1, source_target_pairs={{0,4},{4,8},{8,12},{1,5},{5,9},{9,13},{2,6},{6,10},{10,14},{3,7},{... | collective-permute-start | bytes 7667720 | tf_op jit(solution)/shard_map/ppermute | solution.py:107
  47.9 58.8 %collective-permute-start.1 = (f32[13,64,2,384]{3,1,2,0:T(8,128)S(1)}, f32[13,64,2,384]{3,1,2,0:T(8,128)S(1)}, u32[]{:S(2)}, u32[]{:S(2)}) collective-permute-start(f32[13,64,2,384]{3,1,2,0:T(8,128)S(1)} %get-tuple-element.6), channel_id=1, source_target_pairs={{4,0},{8,4},{12,8},{5,1},{9,5},{13,9},{6,2},{10,6},{14,10},{7,3},{... | collective-permute-start | bytes 7667720 | tf_op jit(solution)/shard_map/ppermute | solution.py:108

commit v2 on v1

v2 whole, which is shorter than its diff:
```python
import functools

import jax
import jax.numpy as jnp
from jax import lax
from jax.experimental import pallas as pl
from jax.experimental.pallas import tpu as pltpu
from jax.sharding import PartitionSpec as P

TAPS = 257
AVG = 10
HALF = TAPS // 2
HALO = -(-HALF // AVG)


def round_up(value, step):
    return -(-value // step) * step


def line_pair(filter_bank, rows, lines):
    summed = sum(
        jnp.pad(filter_bank, ((0, 0), (0, 0), (j, AVG - 1 - j))) for j in range(AVG)
    ) * (1.0 / AVG)
    real, imag = summed[0], summed[1]
    pair = jnp.stack(
        [jnp.stack([real, -imag], axis=-1), jnp.stack([imag, real], axis=-1)], axis=1
    )
    pair = pair.reshape(real.shape[0], 2, 2 * real.shape[1])
    period = round_up(2 * rows + 2 * AVG * lines, 128)
    split = 2 * (AVG * HALO + HALF)
    gap = jnp.zeros(pair.shape[:2] + (period - pair.shape[2],), jnp.float32)
    return jnp.concatenate([pair[:, :, split:], gap, pair[:, :, :split]], axis=2)


def bank_body(lines_ref, flags_ref, bank_ref, *, lines, width):
    for k in range(lines_ref.shape[0]):
        for part in range(2):
            row = lines_ref[k, part : part + 1, :]
            spread = jnp.broadcast_to(row, (8, row.shape[1]))
            tiles = []
            for tile in range(lines // 8):
                shifted = pltpu.roll(spread, 2 * AVG * 8 * tile, 1)
                shifted = pltpu.roll(shifted, 0, 1, stride=AVG, stride_axis=0)
                tiles.append(pltpu.roll(shifted, 0, 1, stride=AVG, stride_axis=0)[:, :width])
            band = jnp.concatenate(tiles, axis=0) * flags_ref[...]
            high = band.astype(jnp.bfloat16)
            low = (band - high.astype(jnp.float32)).astype(jnp.bfloat16)
            bank_ref[k, part * lines : (part + 1) * lines, :] = high
            bank_ref[k, (2 + part) * lines : (3 + part) * lines, :] = low


def main_body(index_ref, vis_ref, bank_ref, out_ref, *, group, half, chunks, chunk):
    first = (pl.program_id(0) * chunks + chunk) * group
    rows, _, _, chans = vis_ref.shape
    for i in range(group):
        band = bank_ref[index_ref[first + i]]
        slab = vis_ref[:, i, :, :].reshape(2 * rows, chans)
        prod = jnp.dot(band, slab, preferred_element_type=jnp.float32)
        out_ref[i] = prod[:half] + prod[half:]


def make_bank(flag_mask, filter_bank, rows):
    kernels = filter_bank.shape[1]
    lines = round_up(rows // AVG + 2 * HALO, 8)
    width = 2 * rows
    pairs = line_pair(filter_bank, rows, lines)
    flags = jnp.repeat(flag_mask.astype(jnp.float32), 2)[None, :]
    per_step = 4 if kernels % 4 == 0 else 1
    return pl.pallas_call(
        functools.partial(bank_body, lines=lines, width=width),
        grid=(kernels // per_step,),
        in_specs=[
            pl.BlockSpec((per_step, 2, pairs.shape[2]), lambda k: (k, 0, 0)),
            pl.BlockSpec((1, width), lambda k: (0, 0)),
        ],
        out_specs=pl.BlockSpec((per_step, 4 * lines, width), lambda k: (k, 0, 0)),
        out_shape=jax.ShapeDtypeStruct((kernels, 4 * lines, width), jnp.bfloat16),
        name="bank",
    )(pairs, flags)


def partial_rows(visibilities, kernel_index, bank, owners, chunks, chunk):
    rows, bases, _, chans = visibilities.shape
    group = bases // owners // chunks
    half = bank.shape[1] // 2
    prod = pl.pallas_call(
        functools.partial(main_body, group=group, half=half, chunks=chunks, chunk=chunk),
        grid_spec=pltpu.PrefetchScalarGridSpec(
            num_scalar_prefetch=1,
            grid=(owners,),
            in_specs=[
                pl.BlockSpec((rows, group, 2, chans), lambda g, _: (0, g * chunks + chunk, 0, 0)),
                pl.BlockSpec(bank.shape, lambda g, _: (0, 0, 0)),
            ],
            out_specs=pl.BlockSpec((group, half, chans), lambda g, _: (g, 0, 0)),
        ),
        out_shape=jax.ShapeDtypeStruct((owners * group, half, chans), jnp.float32),
        compiler_params=pltpu.CompilerParams(vmem_limit_bytes=50 * 1024 * 1024),
        name="partials",
    )(kernel_index, visibilities, bank)
    prod = prod.reshape(owners * group, 2, half // 2, chans)
    return jnp.transpose(prod, (2, 0, 1, 3))


def pack(rows):
    top = jnp.max(jnp.abs(rows), axis=(0, 3), keepdims=True)
    power = jnp.floor(jnp.log2(jnp.maximum(top, 1e-30)))
    scaled = (rows * jnp.exp2(-power)).astype(jnp.float16)
    tail = jnp.broadcast_to(power, (1,) + rows.shape[1:]).astype(jnp.float16)
    return jnp.concatenate([scaled, tail], axis=0)


def unpack(packed):
    wide = packed.astype(jnp.float32)
    return wide[:-1] * jnp.exp2(wide[-1:])


def per_device(visibilities, flag_mask, kernel_index, filter_bank):
    rows, bases, _, chans = visibilities.shape
    own = rows // AVG
    count = lax.axis_size("tm")
    chunks = 2 if (bases // count) % 2 == 0 else 1
    up = [(i, i + 1) for i in range(count - 1)]
    down = [(i + 1, i) for i in range(count - 1)]
    bank = make_bank(flag_mask, filter_bank, rows)
    outputs = []
    for chunk in range(chunks):
        prod = partial_rows(visibilities, kernel_index, bank, count, chunks, chunk)
        from_low = unpack(lax.ppermute(pack(prod[own + HALO : own + 2 * HALO]), "tm", up))
        from_high = unpack(lax.ppermute(pack(prod[:HALO]), "tm", down))
        total = prod[HALO : HALO + own]
        total = total + jnp.pad(from_low, ((0, own - HALO), (0, 0), (0, 0), (0, 0)))
        total = total + jnp.pad(from_high, ((own - HALO, 0), (0, 0), (0, 0), (0, 0)))
        averaged = total.astype(jnp.bfloat16)
        outputs.append(lax.all_to_all(averaged, "tm", split_axis=1, concat_axis=0, tiled=True))
    return jnp.concatenate(outputs, axis=1)


def solution(mesh):
    placed = (
        P(("group", "tm"), ("bl", "pol"), None, None),
        P(("group", "tm")),
        P(("bl", "pol")),
        P(),
    )
    return jax.shard_map(
        per_device,
        mesh=mesh,
        in_specs=placed,
        out_specs=P("group", ("bl", "pol", "tm"), None, None),
        check_vma=False,
    )
```

time: 161 us -> 140 us (0.87)
  blocking collectives: 47.8 us -> 0 us
  starting transfers between devices: 6.59 us -> 23.4 us
  waiting for transfers between devices: 57.3 us -> 44.2 us
  Pallas kernels: 26.5 us -> 38 us
  other arithmetic: 2.76 us -> 12.4 us
  local copies, waits for them, and re-layouts: 19.1 us -> 21.2 us
    ppermute x2 -> x4, waiting for transfers between devices: 57.3 us -> 8.4 us  [the longest x2 7.74 us: per_device(): from_high = unpack(lax.ppermute(pack(prod[:HALO]), 'tm', down))]
    all_to_all x1 -> x0, blocking collectives: 47.8 us -> none  [per_device(): lax.all_to_all(averaged, 'tm', split_axis=1, concat_axis=0, tiled=True)]
    all_to_all x0 -> x2, waiting for transfers between devices: none -> 35.8 us  [per_device(): lax.all_to_all(averaged, 'tm', split_axis=1, concat_axis=0, tiled=True)]
    pallas_call x2 -> x3, Pallas kernels: 26.5 us -> 38 us  [the longest x1 20.3 us: make_bank(): pl.pallas_call(functools.partial(bank_body, lines=lines, width=width), gr...]
    all_to_all x0 -> x2, starting transfers between devices: none -> 9.61 us  [per_device(): lax.all_to_all(averaged, 'tm', split_axis=1, concat_axis=0, tiled=True)]
    ppermute x2 -> x4, starting transfers between devices: 6.59 us -> 13.8 us  [the longest x2 11.2 us: per_device(): lax.ppermute(pack(prod[own + HALO:own + 2 * HALO]), 'tm', up)]
    concatenate x0 -> x5, other arithmetic: none -> 4.53 us  [the longest x1 3.8 us: per_device(): return jnp.concatenate(outputs, axis=1)]
    convert_element_type x1 -> x7, other arithmetic: 0.01 us -> 2.53 us  [the longest x4 1.72 us: unpack(): wide = packed.astype(jnp.float32)]
  transfers between devices with their start and end apart: 2 -> 6, of which waited for: 2 -> 4; matrix products, arithmetic and copies ran while one was open for 0% -> 11% of each run, Pallas kernels for 0% -> 6%
where the time goes in v2:
time: 140 us
  waiting for transfers between devices  44.2 us (32%)
  Pallas kernels  38 us (27%)
  starting transfers between devices  23.4 us (17%)
  local copies, waits for them, and re-layouts  21.2 us (15%)
  other arithmetic  12.4 us (9%)
    all_to_all x2, waiting for transfers between devices, per_device(): lax.all_to_all(averaged, 'tm', split_axis=1, concat_axis=0, tiled=True)  35.8 us
    pallas_call x1, Pallas kernels, make_bank(): pl.pallas_call(functools.partial(bank_body, lines=lines, width=width), gr...  20.3 us
    pallas_call x2, Pallas kernels, partial_rows(): pl.pallas_call(functools.partial(main_body, group=group, half=half, chunk...  17.8 us
    ppermute x2, starting transfers between devices, per_device(): lax.ppermute(pack(prod[own + HALO:own + 2 * HALO]), 'tm', up)  11.2 us
    reshape x2, local copies, waits for them, and re-layouts, partial_rows(): prod = prod.reshape(owners * group, 2, half // 2, chans)  10.1 us
    all_to_all x2, starting transfers between devices, per_device(): lax.all_to_all(averaged, 'tm', split_axis=1, concat_axis=0, tiled=True)  9.61 us
    ppermute x2, waiting for transfers between devices, per_device(): from_high = unpack(lax.ppermute(pack(prod[:HALO]), 'tm', down))  7.74 us
    concatenate x1, other arithmetic, per_device(): return jnp.concatenate(outputs, axis=1)  3.8 us
  transfers between devices with their start and end apart: 6, of which 4 were waited for; matrix products, arithmetic and copies ran while one was open for 11% of the time, Pallas kernels for 6%

profile of v2, /device:TPU:0, one launch (start us, length us, event | category | flops | bytes accessed | tf_op | source)
XLA Modules:
  0.0 139.5 jit_solution(11876900530371880064)
XLA Ops:
  0.0 1.6 %add_multiply_fusion = f32[2,16,266]{2,1,0:T(8,128)S(1)} fusion(f32[2,16,257]{2,1,0:T(8,128)} %param.7), kind=kLoop, calls=%fused_computation.40 | loop fusion | flops 85120 | bytes 66944 | tf_op jit(solution)/shard_map/mul | solution.py:21
  1.6 0.2 copy.15
  1.8 0.2 stack.17
  2.0 0.1 copy.17
  2.1 0.2 copy.16
  2.4 0.2 stack.19
  2.6 0.1 copy.18
  2.7 0.1 pad_maximum_fusion.8
  3.0 0.7 broadcast_in_dim_reshape.3.flags_ref
  3.7 1.1 concatenate.19.lines_ref
  4.8 20.3 %bank.1.bank_ref = bf16[16,192,400]{2,1,0:T(8,128)(2,1)} custom-call(f32[16,2,1408]{2,1,0:T(2,128)} %concatenate.19.lines_ref, f32[1,400]{1,0:T(1,128)} %broadcast_in_dim_reshape.3.flags_ref), custom_call_target="tpu_custom_call" | custom-call | tf_op jit(solution)/shard_map/bank/pallas_call | solution.py:69
  25.1 1.9 %copy-done = bf16[16,192,400]{2,1,0:T(8,128)(2,1)S(1)} copy-done((bf16[16,192,400]{2,1,0:T(8,128)(2,1)S(1)}, bf16[16,192,400]{2,1,0:T(8,128)(2,1)}, u32[]{:S(2)}) %copy-start) | copy-done | bytes 2457624
  27.0 8.9 %partials.3 = f32[32,96,384]{2,1,0:T(8,128)} custom-call(s32[64]{0:T(128)S(1)} %copy-done.1, bf16[200,64,2,384]{3,2,1,0:T(2,128)(2,1)} %vis_ref.3, bf16[16,192,400]{2,1,0:T(8,128)(2,1)S(1)} %copy-done), custom_call_target="tpu_custom_call" | custom-call | tf_op jit(solution)/shard_map/partials/pallas_call | solution.py:86
  35.8 5.1 %copy.27 = f32[32,2,48,384]{3,0,1,2:T(8,128)S(1)} copy(f32[32,2,48,384]{3,2,1,0:T(8,128)} %bitcast.41) | data formatting | bytes 9437184 | tf_op jit(solution)/shard_map/reshape | solution.py:101
  40.9 0.3 abs_reduce_fusion.1
  41.2 0.4 multiply_convert_fusion.1
  41.7 0.2 pad_maximum_fusion.4
  41.9 1.3 collective-permute-start.3
  43.3 0.2 pad_maximum_fusion.3
  43.4 5.8 %collective-permute-start.2 = (f16[14,32,2,384]{3,1,2,0:T(8,128)(2,1)S(1)}, f16[14,32,2,384]{3,1,2,0:T(8,128)(2,1)S(1)}, u32[]{:S(2)}, u32[]{:S(2)}) collective-permute-start(f16[14,32,2,384]{3,1,2,0:T(8,128)(2,1)S(1)} %pad_maximum_fusion.3), channel_id=1, source_target_pairs={{0,4},{4,8},{8,12},{1,5},{5,9},{9,13},{2,6},{6,10},{10,14},{3,7},{... | collective-permute-start | bytes 2064392 | tf_op jit(solution)/shard_map/ppermute | solution.py:129
  49.3 8.9 %partials.2 = f32[32,96,384]{2,1,0:T(8,128)} custom-call(s32[64]{0:T(128)S(1)} %copy-done.1, bf16[200,64,2,384]{3,2,1,0:T(2,128)(2,1)} %vis_ref.3, bf16[16,192,400]{2,1,0:T(8,128)(2,1)S(1)} %copy-done), custom_call_target="tpu_custom_call" | custom-call | tf_op jit(solution)/shard_map/partials/pallas_call | solution.py:86
  58.1 5.1 %copy.28 = f32[32,2,48,384]{3,0,1,2:T(8,128)S(1)} copy(f32[32,2,48,384]{3,2,1,0:T(8,128)} %bitcast.40) | data formatting | bytes 9437184 | tf_op jit(solution)/shard_map/reshape | solution.py:101
  63.2 0.3 abs_reduce_fusion.3
  63.5 0.4 multiply_convert_fusion.3
  64.0 0.2 pad_maximum_fusion.2
  64.2 1.1 copy-done.2
  65.4 1.3 collective-permute-start.1
  66.7 0.2 pad_maximum_fusion.1
  66.9 5.4 %collective-permute-start = (f16[14,32,2,384]{3,1,2,0:T(8,128)(2,1)S(1)}, f16[14,32,2,384]{3,1,2,0:T(8,128)(2,1)}, u32[]{:S(2)}, u32[]{:S(2)}) collective-permute-start(f16[14,32,2,384]{3,1,2,0:T(8,128)(2,1)S(1)} %pad_maximum_fusion.1), channel_id=1, source_target_pairs={{0,4},{4,8},{8,12},{1,5},{5,9},{9,13},{2,6},{6,10},{10,14},{3,7},{... | collective-permute-start | bytes 2064392 | tf_op jit(solution)/shard_map/ppermute | solution.py:129
  72.3 0.2 convert_element_type.108
  72.5 0.1 slice_multiply_fusion
  72.6 0.2 convert_element_type.105
  73.0 0.5 fusion.1
  73.5 1.7 %copy.23 = bf16[20,32,2,384]{3,2,0,1:T(2,128)(2,1)} copy(bf16[20,32,2,384]{3,1,2,0:T(8,128)(2,1)S(1)} %fusion.1) | data formatting | bytes 1966080 | tf_op jit(solution)/shard_map/convert_element_type | solution.py:134
  75.2 3.5 %all-to-all-start.1 = ((bf16[20,32,2,384]{3,2,0,1:T(2,128)(2,1)}), bf16[20,32,2,384]{3,2,0,1:T(2,128)(2,1)S(1)}, u32[]{:S(2)}, u32[]{:S(2)}) async-start(bf16[20,32,2,384]{3,2,0,1:T(2,128)(2,1)} %copy.23), calls=%async_computation.1 | async-start | bytes 1966080 | tf_op jit(solution)/shard_map/all_to_all | solution.py:135
  78.7 7.7 %collective-permute-done.1 = f16[14,32,2,384]{3,1,2,0:T(8,128)(2,1)S(1)} collective-permute-done((f16[14,32,2,384]{3,1,2,0:T(8,128)(2,1)S(1)}, f16[14,32,2,384]{3,1,2,0:T(8,128)(2,1)S(1)}, u32[]{:S(2)}, u32[]{:S(2)}) %collective-permute-start.1) | collective-permute-done | bytes 688160 | tf_op jit(solution)/shard_map/ppermute | solution.py:130
  86.5 0.2 convert_element_type.101
  86.6 0.7 collective-permute-done
  87.3 1.3 convert_element_type.98
  88.6 0.1 slice_multiply_fusion.2
  88.8 2.0 %fusion.3 = bf16[20,32,2,384]{3,1,2,0:T(8,128)(2,1)S(1)} fusion(f32[48,32,2,384]{3,1,2,0:T(8,128)} %bitcast.39, f32[13,32,2,384]{3,1,2,0:T(8,128)S(1)} %slice_multiply_fusion.2, f32[13,32,2,384]{3,1,2,0:T(8,128)S(1)} %slice_multiply_fusion.3), kind=kLoop, calls=%fused_computation.7 | loop fusion | flops 1474560 | bytes 5505024 | tf_op jit(solution)/shard_map/convert_element_type | solution.py:134
  90.8 1.7 %copy.20 = bf16[20,32,2,384]{3,2,0,1:T(2,128)(2,1)} copy(bf16[20,32,2,384]{3,1,2,0:T(8,128)(2,1)S(1)} %fusion.3) | data formatting | bytes 1966080 | tf_op jit(solution)/shard_map/convert_element_type | solution.py:134
  92.5 13.8 %all-to-all-done.1 = bf16[20,32,2,384]{3,2,0,1:T(2,128)(2,1)S(1)} async-done(((bf16[20,32,2,384]{3,2,0,1:T(2,128)(2,1)}), bf16[20,32,2,384]{3,2,0,1:T(2,128)(2,1)S(1)}, u32[]{:S(2)}, u32[]{:S(2)}) %all-to-all-start.1) | async-done | bytes 983072 | tf_op jit(solution)/shard_map/all_to_all | solution.py:135
  106.3 6.1 %all-to-all-start = ((bf16[20,32,2,384]{3,2,0,1:T(2,128)(2,1)}), bf16[20,32,2,384]{3,2,0,1:T(2,128)(2,1)S(1)}, u32[]{:S(2)}, u32[]{:S(2)}) async-start(bf16[20,32,2,384]{3,2,0,1:T(2,128)(2,1)} %copy.20), calls=%async_computation | async-start | bytes 1966080 | tf_op jit(solution)/shard_map/all_to_all | solution.py:135
  112.4 0.7 copy.24
  113.1 21.9 %all-to-all-done = bf16[20,32,2,384]{3,2,0,1:T(2,128)(2,1)S(1)} async-done(((bf16[20,32,2,384]{3,2,0,1:T(2,128)(2,1)}), bf16[20,32,2,384]{3,2,0,1:T(2,128)(2,1)S(1)}, u32[]{:S(2)}, u32[]{:S(2)}) %all-to-all-start) | async-done | bytes 983072 | tf_op jit(solution)/shard_map/all_to_all | solution.py:135
  135.1 0.7 copy.21
  135.7 3.8 %pad_maximum_fusion = bf16[80,16,2,384]{3,2,1,0:T(2,128)(2,1)} fusion(bf16[80,8,2,384]{3,2,1,0:T(2,128)(2,1)S(1)} %bitcast.44, bf16[80,8,2,384]{3,2,1,0:T(2,128)(2,1)S(1)} %bitcast.45), kind=kLoop, calls=%fused_computation.8 | loop fusion | flops 983040 | bytes 3932160 | tf_op jit(solution)/shard_map/concatenate | solution.py:136
  (27 shorter events, 0.9 us)
Async XLA Ops:
  1.6 1.3 copy-start.3
  4.8 20.3 %copy-start.1 = (s32[64]{0:T(128)S(1)}, s32[64]{0:T(128)}, u32[]{:S(2)}) copy-start(s32[64]{0:T(128)} %index_ref.3) | copy-start | bytes 772
  25.1 1.9 %copy-start = (bf16[16,192,400]{2,1,0:T(8,128)(2,1)S(1)}, bf16[16,192,400]{2,1,0:T(8,128)(2,1)}, u32[]{:S(2)}) copy-start(bf16[16,192,400]{2,1,0:T(8,128)(2,1)} %bank.1.bank_ref) | copy-start | bytes 7372804
  41.9 30.4 %collective-permute-start.3 = (f16[14,32,2,384]{3,1,2,0:T(8,128)(2,1)S(1)}, f16[14,32,2,384]{3,1,2,0:T(8,128)(2,1)S(1)}, u32[]{:S(2)}, u32[]{:S(2)}) collective-permute-start(f16[14,32,2,384]{3,1,2,0:T(8,128)(2,1)S(1)} %pad_maximum_fusion.4), channel_id=1, source_target_pairs={{4,0},{8,4},{12,8},{5,1},{9,5},{13,9},{6,2},{10,6},{14,10},{7,3},{... | collective-permute-start | bytes 2064392 | tf_op jit(solution)/shard_map/ppermute | solution.py:130
  43.4 29.2 %collective-permute-start.2 = (f16[14,32,2,384]{3,1,2,0:T(8,128)(2,1)S(1)}, f16[14,32,2,384]{3,1,2,0:T(8,128)(2,1)S(1)}, u32[]{:S(2)}, u32[]{:S(2)}) collective-permute-start(f16[14,32,2,384]{3,1,2,0:T(8,128)(2,1)S(1)} %pad_maximum_fusion.3), channel_id=1, source_target_pairs={{0,4},{4,8},{8,12},{1,5},{5,9},{9,13},{2,6},{6,10},{10,14},{3,7},{... | collective-permute-start | bytes 2064392 | tf_op jit(solution)/shard_map/ppermute | solution.py:129
  63.2 2.1 %copy-start.2 = (f32[32,2,48,384]{3,0,1,2:T(8,128)}, f32[32,2,48,384]{3,0,1,2:T(8,128)S(1)}, u32[]{:S(2)}) copy-start(f32[32,2,48,384]{3,0,1,2:T(8,128)S(1)} %copy.28) | copy-start | bytes 14155780
  65.4 21.1 %collective-permute-start.1 = (f16[14,32,2,384]{3,1,2,0:T(8,128)(2,1)S(1)}, f16[14,32,2,384]{3,1,2,0:T(8,128)(2,1)S(1)}, u32[]{:S(2)}, u32[]{:S(2)}) collective-permute-start(f16[14,32,2,384]{3,1,2,0:T(8,128)(2,1)S(1)} %pad_maximum_fusion.2), channel_id=1, source_target_pairs={{4,0},{8,4},{12,8},{5,1},{9,5},{13,9},{6,2},{10,6},{14,10},{7,3},{... | collective-permute-start | bytes 2064392 | tf_op jit(solution)/shard_map/ppermute | solution.py:130
  66.9 20.4 %collective-permute-start = (f16[14,32,2,384]{3,1,2,0:T(8,128)(2,1)S(1)}, f16[14,32,2,384]{3,1,2,0:T(8,128)(2,1)}, u32[]{:S(2)}, u32[]{:S(2)}) collective-permute-start(f16[14,32,2,384]{3,1,2,0:T(8,128)(2,1)S(1)} %pad_maximum_fusion.1), channel_id=1, source_target_pairs={{0,4},{4,8},{8,12},{1,5},{5,9},{9,13},{2,6},{6,10},{10,14},{3,7},{... | collective-permute-start | bytes 2064392 | tf_op jit(solution)/shard_map/ppermute | solution.py:129
  75.2 31.1 %all-to-all-start.1 = ((bf16[20,32,2,384]{3,2,0,1:T(2,128)(2,1)}), bf16[20,32,2,384]{3,2,0,1:T(2,128)(2,1)S(1)}, u32[]{:S(2)}, u32[]{:S(2)}) async-start(bf16[20,32,2,384]{3,2,0,1:T(2,128)(2,1)} %copy.23), calls=%async_computation.1 | async-start | bytes 1966080 | tf_op jit(solution)/shard_map/all_to_all | solution.py:135
  106.3 28.7 %all-to-all-start = ((bf16[20,32,2,384]{3,2,0,1:T(2,128)(2,1)}), bf16[20,32,2,384]{3,2,0,1:T(2,128)(2,1)S(1)}, u32[]{:S(2)}, u32[]{:S(2)}) async-start(bf16[20,32,2,384]{3,2,0,1:T(2,128)(2,1)} %copy.20), calls=%async_computation | async-start | bytes 1966080 | tf_op jit(solution)/shard_map/all_to_all | solution.py:135

commit v3 on v2

--- a/solution.py
+++ b/solution.py
@@ -33,6 +33,8 @@
 
 
 def bank_body(lines_ref, flags_ref, bank_ref, *, lines, width):
+    head = round_up(width, 128)
+    tail = round_up(2 * AVG * 8, 128)
     for k in range(lines_ref.shape[0]):
         for part in range(2):
             row = lines_ref[k, part : part + 1, :]
@@ -40,6 +42,7 @@
             tiles = []
             for tile in range(lines // 8):
                 shifted = pltpu.roll(spread, 2 * AVG * 8 * tile, 1)
+                shifted = jnp.concatenate([shifted[:, :head], shifted[:, -tail:]], axis=1)
                 shifted = pltpu.roll(shifted, 0, 1, stride=AVG, stride_axis=0)
                 tiles.append(pltpu.roll(shifted, 0, 1, stride=AVG, stride_axis=0)[:, :width])
             band = jnp.concatenate(tiles, axis=0) * flags_ref[...]
@@ -65,7 +68,7 @@
     width = 2 * rows
     pairs = line_pair(filter_bank, rows, lines)
     flags = jnp.repeat(flag_mask.astype(jnp.float32), 2)[None, :]
-    per_step = 4 if kernels % 4 == 0 else 1
+    per_step = 1
     return pl.pallas_call(
         functools.partial(bank_body, lines=lines, width=width),
         grid=(kernels // per_step,),

time: 140 us -> 131 us (0.936)
  Pallas kernels: 38 us -> 28.3 us
    pallas_call x1, Pallas kernels: 20.3 us -> 10.5 us  [make_bank(): pl.pallas_call(functools.partial(bank_body, lines=lines, width=width), gr...]
  transfers between devices with their start and end apart: 6 -> 6, of which waited for: 4 -> 4; matrix products, arithmetic and copies ran while one was open for 11% -> 12% of each run, Pallas kernels for 6% -> 7%
where the time goes in v3:
time: 131 us; the launch traced here: 130 us
  waiting for transfers between devices  44 us (34%)
  Pallas kernels  28.3 us (22%)
  starting transfers between devices  23.6 us (18%)
  local copies, waits for them, and re-layouts  21.2 us (16%)
  other arithmetic  12.4 us (9%)
    all_to_all x2, waiting for transfers between devices, per_device(): lax.all_to_all(averaged, 'tm', split_axis=1, concat_axis=0, tiled=True)  35.6 us
    pallas_call x2, Pallas kernels, partial_rows(): pl.pallas_call(functools.partial(main_body, group=group, half=half, chunk...  17.8 us
    ppermute x2, starting transfers between devices, per_device(): lax.ppermute(pack(prod[own + HALO:own + 2 * HALO]), 'tm', up)  11 us
    pallas_call x1, Pallas kernels, make_bank(): pl.pallas_call(functools.partial(bank_body, lines=lines, width=width), gr...  10.5 us
    reshape x2, local copies, waits for them, and re-layouts, partial_rows(): prod = prod.reshape(owners * group, 2, half // 2, chans)  10.1 us
    all_to_all x2, starting transfers between devices, per_device(): lax.all_to_all(averaged, 'tm', split_axis=1, concat_axis=0, tiled=True)  9.79 us
    ppermute x2, waiting for transfers between devices, per_device(): from_high = unpack(lax.ppermute(pack(prod[:HALO]), 'tm', down))  7.57 us
    concatenate x1, other arithmetic, per_device(): return jnp.concatenate(outputs, axis=1)  3.8 us
  transfers between devices with their start and end apart: 6, of which 4 were waited for; matrix products, arithmetic and copies ran while one was open for 12% of the time, Pallas kernels for 7%

profile of v3, /device:TPU:0, one launch (start us, length us, event | category | flops | bytes accessed | tf_op | source)
XLA Modules:
  0.0 129.8 jit_solution(1847890435382473982)
XLA Ops:
  0.0 1.6 %add_multiply_fusion = f32[2,16,266]{2,1,0:T(8,128)S(1)} fusion(f32[2,16,257]{2,1,0:T(8,128)} %param.7), kind=kLoop, calls=%fused_computation.40 | loop fusion | flops 85120 | bytes 66944 | tf_op jit(solution)/shard_map/mul | solution.py:21
  1.6 0.2 copy.15
  1.8 0.2 stack.17
  2.0 0.1 copy.17
  2.1 0.2 copy.16
  2.4 0.2 stack.19
  2.6 0.1 copy.18
  2.7 0.1 pad_maximum_fusion.8
  3.0 0.7 broadcast_in_dim_reshape.3.flags_ref
  3.7 1.1 concatenate.19.lines_ref
  4.8 10.5 %bank.1.bank_ref = bf16[16,192,400]{2,1,0:T(8,128)(2,1)} custom-call(f32[16,2,1408]{2,1,0:T(2,128)} %concatenate.19.lines_ref, f32[1,400]{1,0:T(1,128)} %broadcast_in_dim_reshape.3.flags_ref), custom_call_target="tpu_custom_call" | custom-call | tf_op jit(solution)/shard_map/bank/pallas_call | solution.py:72
  15.3 1.9 %copy-done = bf16[16,192,400]{2,1,0:T(8,128)(2,1)S(1)} copy-done((bf16[16,192,400]{2,1,0:T(8,128)(2,1)S(1)}, bf16[16,192,400]{2,1,0:T(8,128)(2,1)}, u32[]{:S(2)}) %copy-start) | copy-done | bytes 2457624
  17.2 8.9 %partials.3 = f32[32,96,384]{2,1,0:T(8,128)} custom-call(s32[64]{0:T(128)S(1)} %copy-done.1, bf16[200,64,2,384]{3,2,1,0:T(2,128)(2,1)} %vis_ref.3, bf16[16,192,400]{2,1,0:T(8,128)(2,1)S(1)} %copy-done), custom_call_target="tpu_custom_call" | custom-call | tf_op jit(solution)/shard_map/partials/pallas_call | solution.py:89
  26.1 5.1 %copy.27 = f32[32,2,48,384]{3,0,1,2:T(8,128)S(1)} copy(f32[32,2,48,384]{3,2,1,0:T(8,128)} %bitcast.41) | data formatting | bytes 9437184 | tf_op jit(solution)/shard_map/reshape | solution.py:104
  31.2 0.3 abs_reduce_fusion.1
  31.5 0.4 multiply_convert_fusion.1
  32.0 0.2 pad_maximum_fusion.4
  32.1 1.3 collective-permute-start.3
  33.5 0.2 pad_maximum_fusion.3
  33.7 5.6 %collective-permute-start.2 = (f16[14,32,2,384]{3,1,2,0:T(8,128)(2,1)S(1)}, f16[14,32,2,384]{3,1,2,0:T(8,128)(2,1)S(1)}, u32[]{:S(2)}, u32[]{:S(2)}) collective-permute-start(f16[14,32,2,384]{3,1,2,0:T(8,128)(2,1)S(1)} %pad_maximum_fusion.3), channel_id=1, source_target_pairs={{0,4},{4,8},{8,12},{1,5},{5,9},{9,13},{2,6},{6,10},{10,14},{3,7},{... | collective-permute-start | bytes 2064392 | tf_op jit(solution)/shard_map/ppermute | solution.py:132
  39.3 8.9 %partials.2 = f32[32,96,384]{2,1,0:T(8,128)} custom-call(s32[64]{0:T(128)S(1)} %copy-done.1, bf16[200,64,2,384]{3,2,1,0:T(2,128)(2,1)} %vis_ref.3, bf16[16,192,400]{2,1,0:T(8,128)(2,1)S(1)} %copy-done), custom_call_target="tpu_custom_call" | custom-call | tf_op jit(solution)/shard_map/partials/pallas_call | solution.py:89
  48.2 5.1 %copy.28 = f32[32,2,48,384]{3,0,1,2:T(8,128)S(1)} copy(f32[32,2,48,384]{3,2,1,0:T(8,128)} %bitcast.40) | data formatting | bytes 9437184 | tf_op jit(solution)/shard_map/reshape | solution.py:104
  53.3 0.3 abs_reduce_fusion.3
  53.6 0.4 multiply_convert_fusion.3
  54.1 0.2 pad_maximum_fusion.2
  54.3 1.1 copy-done.2
  55.4 1.5 %collective-permute-start.1 = (f16[14,32,2,384]{3,1,2,0:T(8,128)(2,1)S(1)}, f16[14,32,2,384]{3,1,2,0:T(8,128)(2,1)S(1)}, u32[]{:S(2)}, u32[]{:S(2)}) collective-permute-start(f16[14,32,2,384]{3,1,2,0:T(8,128)(2,1)S(1)} %pad_maximum_fusion.2), channel_id=1, source_target_pairs={{4,0},{8,4},{12,8},{5,1},{9,5},{13,9},{6,2},{10,6},{14,10},{7,3},{... | collective-permute-start | bytes 2064392 | tf_op jit(solution)/shard_map/ppermute | solution.py:133
  57.0 0.2 pad_maximum_fusion.1
  57.2 5.4 %collective-permute-start = (f16[14,32,2,384]{3,1,2,0:T(8,128)(2,1)S(1)}, f16[14,32,2,384]{3,1,2,0:T(8,128)(2,1)}, u32[]{:S(2)}, u32[]{:S(2)}) collective-permute-start(f16[14,32,2,384]{3,1,2,0:T(8,128)(2,1)S(1)} %pad_maximum_fusion.1), channel_id=1, source_target_pairs={{0,4},{4,8},{8,12},{1,5},{5,9},{9,13},{2,6},{6,10},{10,14},{3,7},{... | collective-permute-start | bytes 2064392 | tf_op jit(solution)/shard_map/ppermute | solution.py:132
  62.6 0.2 convert_element_type.108
  62.8 0.1 slice_multiply_fusion
  62.9 0.2 convert_element_type.105
  63.2 0.5 fusion.1
  63.7 1.7 %copy.23 = bf16[20,32,2,384]{3,2,0,1:T(2,128)(2,1)} copy(bf16[20,32,2,384]{3,1,2,0:T(8,128)(2,1)S(1)} %fusion.1) | data formatting | bytes 1966080 | tf_op jit(solution)/shard_map/convert_element_type | solution.py:137
  65.5 3.5 %all-to-all-start.1 = ((bf16[20,32,2,384]{3,2,0,1:T(2,128)(2,1)}), bf16[20,32,2,384]{3,2,0,1:T(2,128)(2,1)S(1)}, u32[]{:S(2)}, u32[]{:S(2)}) async-start(bf16[20,32,2,384]{3,2,0,1:T(2,128)(2,1)} %copy.23), calls=%async_computation.1 | async-start | bytes 1966080 | tf_op jit(solution)/shard_map/all_to_all | solution.py:138
  69.0 7.6 %collective-permute-done.1 = f16[14,32,2,384]{3,1,2,0:T(8,128)(2,1)S(1)} collective-permute-done((f16[14,32,2,384]{3,1,2,0:T(8,128)(2,1)S(1)}, f16[14,32,2,384]{3,1,2,0:T(8,128)(2,1)S(1)}, u32[]{:S(2)}, u32[]{:S(2)}) %collective-permute-start.1) | collective-permute-done | bytes 688160 | tf_op jit(solution)/shard_map/ppermute | solution.py:133
  76.5 0.2 convert_element_type.101
  76.7 0.8 collective-permute-done
  77.5 1.3 convert_element_type.98
  78.9 0.1 slice_multiply_fusion.2
  79.1 2.0 %fusion.3 = bf16[20,32,2,384]{3,1,2,0:T(8,128)(2,1)S(1)} fusion(f32[48,32,2,384]{3,1,2,0:T(8,128)} %bitcast.39, f32[13,32,2,384]{3,1,2,0:T(8,128)S(1)} %slice_multiply_fusion.2, f32[13,32,2,384]{3,1,2,0:T(8,128)S(1)} %slice_multiply_fusion.3), kind=kLoop, calls=%fused_computation.7 | loop fusion | flops 1474560 | bytes 5505024 | tf_op jit(solution)/shard_map/convert_element_type | solution.py:137
  81.1 1.7 %copy.20 = bf16[20,32,2,384]{3,2,0,1:T(2,128)(2,1)} copy(bf16[20,32,2,384]{3,1,2,0:T(8,128)(2,1)S(1)} %fusion.3) | data formatting | bytes 1966080 | tf_op jit(solution)/shard_map/convert_element_type | solution.py:137
  82.8 13.7 %all-to-all-done.1 = bf16[20,32,2,384]{3,2,0,1:T(2,128)(2,1)S(1)} async-done(((bf16[20,32,2,384]{3,2,0,1:T(2,128)(2,1)}), bf16[20,32,2,384]{3,2,0,1:T(2,128)(2,1)S(1)}, u32[]{:S(2)}, u32[]{:S(2)}) %all-to-all-start.1) | async-done | bytes 983072 | tf_op jit(solution)/shard_map/all_to_all | solution.py:138
  96.4 6.3 %all-to-all-start = ((bf16[20,32,2,384]{3,2,0,1:T(2,128)(2,1)}), bf16[20,32,2,384]{3,2,0,1:T(2,128)(2,1)S(1)}, u32[]{:S(2)}, u32[]{:S(2)}) async-start(bf16[20,32,2,384]{3,2,0,1:T(2,128)(2,1)} %copy.20), calls=%async_computation | async-start | bytes 1966080 | tf_op jit(solution)/shard_map/all_to_all | solution.py:138
  102.7 0.7 copy.24
  103.4 21.9 %all-to-all-done = bf16[20,32,2,384]{3,2,0,1:T(2,128)(2,1)S(1)} async-done(((bf16[20,32,2,384]{3,2,0,1:T(2,128)(2,1)}), bf16[20,32,2,384]{3,2,0,1:T(2,128)(2,1)S(1)}, u32[]{:S(2)}, u32[]{:S(2)}) %all-to-all-start) | async-done | bytes 983072 | tf_op jit(solution)/shard_map/all_to_all | solution.py:138
  125.3 0.7 copy.21
  126.0 3.8 %pad_maximum_fusion = bf16[80,16,2,384]{3,2,1,0:T(2,128)(2,1)} fusion(bf16[80,8,2,384]{3,2,1,0:T(2,128)(2,1)S(1)} %bitcast.44, bf16[80,8,2,384]{3,2,1,0:T(2,128)(2,1)S(1)} %bitcast.45), kind=kLoop, calls=%fused_computation.8 | loop fusion | flops 983040 | bytes 3932160 | tf_op jit(solution)/shard_map/concatenate | solution.py:139
  (27 shorter events, 0.9 us)
Async XLA Ops:
  1.6 1.3 copy-start.3
  4.8 10.5 %copy-start.1 = (s32[64]{0:T(128)S(1)}, s32[64]{0:T(128)}, u32[]{:S(2)}) copy-start(s32[64]{0:T(128)} %index_ref.3) | copy-start | bytes 772
  15.3 1.9 %copy-start = (bf16[16,192,400]{2,1,0:T(8,128)(2,1)S(1)}, bf16[16,192,400]{2,1,0:T(8,128)(2,1)}, u32[]{:S(2)}) copy-start(bf16[16,192,400]{2,1,0:T(8,128)(2,1)} %bank.1.bank_ref) | copy-start | bytes 7372804
  32.1 30.4 %collective-permute-start.3 = (f16[14,32,2,384]{3,1,2,0:T(8,128)(2,1)S(1)}, f16[14,32,2,384]{3,1,2,0:T(8,128)(2,1)S(1)}, u32[]{:S(2)}, u32[]{:S(2)}) collective-permute-start(f16[14,32,2,384]{3,1,2,0:T(8,128)(2,1)S(1)} %pad_maximum_fusion.4), channel_id=1, source_target_pairs={{4,0},{8,4},{12,8},{5,1},{9,5},{13,9},{6,2},{10,6},{14,10},{7,3},{... | collective-permute-start | bytes 2064392 | tf_op jit(solution)/shard_map/ppermute | solution.py:133
  33.7 29.2 %collective-permute-start.2 = (f16[14,32,2,384]{3,1,2,0:T(8,128)(2,1)S(1)}, f16[14,32,2,384]{3,1,2,0:T(8,128)(2,1)S(1)}, u32[]{:S(2)}, u32[]{:S(2)}) collective-permute-start(f16[14,32,2,384]{3,1,2,0:T(8,128)(2,1)S(1)} %pad_maximum_fusion.3), channel_id=1, source_target_pairs={{0,4},{4,8},{8,12},{1,5},{5,9},{9,13},{2,6},{6,10},{10,14},{3,7},{... | collective-permute-start | bytes 2064392 | tf_op jit(solution)/shard_map/ppermute | solution.py:132
  53.3 2.1 %copy-start.2 = (f32[32,2,48,384]{3,0,1,2:T(8,128)}, f32[32,2,48,384]{3,0,1,2:T(8,128)S(1)}, u32[]{:S(2)}) copy-start(f32[32,2,48,384]{3,0,1,2:T(8,128)S(1)} %copy.28) | copy-start | bytes 14155780
  55.4 21.1 %collective-permute-start.1 = (f16[14,32,2,384]{3,1,2,0:T(8,128)(2,1)S(1)}, f16[14,32,2,384]{3,1,2,0:T(8,128)(2,1)S(1)}, u32[]{:S(2)}, u32[]{:S(2)}) collective-permute-start(f16[14,32,2,384]{3,1,2,0:T(8,128)(2,1)S(1)} %pad_maximum_fusion.2), channel_id=1, source_target_pairs={{4,0},{8,4},{12,8},{5,1},{9,5},{13,9},{6,2},{10,6},{14,10},{7,3},{... | collective-permute-start | bytes 2064392 | tf_op jit(solution)/shard_map/ppermute | solution.py:133
  57.2 20.4 %collective-permute-start = (f16[14,32,2,384]{3,1,2,0:T(8,128)(2,1)S(1)}, f16[14,32,2,384]{3,1,2,0:T(8,128)(2,1)}, u32[]{:S(2)}, u32[]{:S(2)}) collective-permute-start(f16[14,32,2,384]{3,1,2,0:T(8,128)(2,1)S(1)} %pad_maximum_fusion.1), channel_id=1, source_target_pairs={{0,4},{4,8},{8,12},{1,5},{5,9},{9,13},{2,6},{6,10},{10,14},{3,7},{... | collective-permute-start | bytes 2064392 | tf_op jit(solution)/shard_map/ppermute | solution.py:132
  65.5 31.0 %all-to-all-start.1 = ((bf16[20,32,2,384]{3,2,0,1:T(2,128)(2,1)}), bf16[20,32,2,384]{3,2,0,1:T(2,128)(2,1)S(1)}, u32[]{:S(2)}, u32[]{:S(2)}) async-start(bf16[20,32,2,384]{3,2,0,1:T(2,128)(2,1)} %copy.23), calls=%async_computation.1 | async-start | bytes 1966080 | tf_op jit(solution)/shard_map/all_to_all | solution.py:138
  96.4 28.9 %all-to-all-start = ((bf16[20,32,2,384]{3,2,0,1:T(2,128)(2,1)}), bf16[20,32,2,384]{3,2,0,1:T(2,128)(2,1)S(1)}, u32[]{:S(2)}, u32[]{:S(2)}) async-start(bf16[20,32,2,384]{3,2,0,1:T(2,128)(2,1)} %copy.20), calls=%async_computation | async-start | bytes 1966080 | tf_op jit(solution)/shard_map/all_to_all | solution.py:138
